TPU v7x, 32 devices: a whole 2x2x4 slice. The times are simulated.
32 devices in a mesh: ga: 8 (over z, x), ta: 4 (over y, core).
Axes of the slice: x: 2, y: 2, z: 4, core: 2. Of those that a mesh axis runs over, the one named last changes fastest.
Arguments:
- density: bfloat16 [2, 6144, 16384], P(None, 'ga', 'ta'), may hold values from -6 to 6
- coulomb: float32 [6144], P('ga'), may hold values from 0.001275776 to 0.01275776
- row_block: int32 [1], replicated, may hold values from 0 to 67
Outputs:
- kernel: float32 [4, 4096, 2, 240], P('ta', 'ga')
Inputs may be any that keep to these rules, and one draw needn't show every extreme that they name: The rows row_block * 240 to row_block * 240 + 239 lie among the 16384 transitions.
All inputs are finite; a program needn't handle non-finite values.
Results may differ from a plain program's by a relative error of at most 0.0025.
Values may be sent and summed in bfloat16 or wider, within the bound.
A program may use at most 64 MiB of HBM per device.

v0:
```python
import jax
import jax.numpy as jnp
from jax import lax
from jax.sharding import PartitionSpec as P

RB = 240


def stack_left(folded):
    real_part = folded[0]
    imag_part = folded[1]
    upper_half = jnp.concatenate([real_part, -imag_part], axis=1)
    lower_half = jnp.concatenate([imag_part, real_part], axis=1)
    return jnp.concatenate([upper_half, lower_half], axis=0)


def body(density, coulomb, row_block):
    local_g = density.shape[1]
    col_width = density.shape[2]
    group_index = lax.axis_index("ta")
    column = row_block[0] * RB + jnp.arange(RB, dtype=jnp.int32)
    owner_index = column // col_width
    position = jnp.clip(column - group_index * col_width, 0, col_width - 1)
    picked = jnp.take(density, position, axis=2)
    weighted = (coulomb[None, :, None] * picked.astype(jnp.float32)).astype(jnp.bfloat16)
    masked = jnp.where(
        (owner_index == group_index)[None, None, :], weighted.astype(jnp.float32), 0.0
    )
    folded = lax.psum(masked.astype(jnp.bfloat16), "ta")
    stacked = stack_left(folded)
    own_rows = col_width // lax.axis_size("ga")
    sliced = density.reshape(2 * local_g, lax.axis_size("ga") * own_rows)
    kernel = lax.psum_scatter(
        lax.dot_general(
            sliced, stacked, (((0,), (0,)), ((), ())), preferred_element_type=jnp.float32
        ),
        "ga",
        scatter_dimension=0,
        tiled=True,
    )
    return kernel.reshape(1, kernel.shape[0], 2, RB)


def solution(mesh):
    in_specs = (P(None, "ga", "ta"), P("ga"), P())
    out_specs = P("ta", "ga", None, None)
    return jax.shard_map(body, mesh=mesh, in_specs=in_specs, out_specs=out_specs, check_vma=False)
```

profile of v0, /device:TPU:0, one launch (start us, length us, event | category | flops | bytes accessed | tf_op | source)
XLA Modules:
  0.0 247.2 jit_solution(10812116345461376397)
XLA Ops:
  6.5 0.0 all-reduce.2.cloned.1.call-start
  7.2 0.0 copy-start
  7.3 31.4 %copy.7 = bf16[2,768,4096]{1,0,2:T(2,128)(2,1)} copy(bf16[2,768,4096]{2,1,0:T(8,128)(2,1)} %param.3) | data formatting | bytes 25165824 | tf_op args[0]
  38.6 6.8 %gather_fusion = bf16[240,2,768]{2,1,0:T(2,128)(2,1)S(1)} fusion(bf16[2,768,4096]{1,0,2:T(2,128)(2,1)} %copy.7, s32[1024]{0:T(1024)S(1)} %pad_clamp_fusion), kind=kCustom, calls=%fused_computation | custom fusion | bytes 1475520 | tf_op jit(solution)/shard_map/jit(_take)/gather | solution.py:24
  45.4 0.0 copy-done
  45.4 2.5 %fusion.7 = bf16[2,768,240]{1,0,2:T(2,128)(2,1)} fusion(bf16[240,2,768]{2,1,0:T(2,128)(2,1)S(1)} %gather_fusion, pred[240]{0:T(512)(128)(4,1)S(1)} %get-tuple-element.9, f32[768]{0:T(1024)S(1)} %copy-done, pred[240]{0:T(512)(128)(4,1)S(1)} %get-tuple-element.10), kind=kLoop, calls=%fused_computation.12 | loop fusion | flops 2580480 | bytes 1478112 | tf_op jit(solution)/shard_map/convert_element_type | solution.py:29
  47.9 0.0 all-reduce.2.cloned.1.call-update
  48.0 0.0 reduce-scatter.2.cloned.1.call-start
  48.0 37.2 %all-reduce.2.cloned.1.call-done = bf16[2,768,240]{1,0,2:T(2,128)(2,1)} async-done(((bf16[2,768,240]{1,0,2:T(2,128)(2,1)}), bf16[2,768,240]{1,0,2:T(2,128)(2,1)}) %all-reduce.2.cloned.1.call-update) | async-done | bytes 737296 | tf_op jit(solution)/shard_map/psum | solution.py:29
  85.3 2.6 %fusion.11 = (bf16[1,768,240]{1,0,2:T(2,128)(2,1)S(1)}, bf16[1,768,240]{1,0,2:T(2,128)(2,1)S(1)}) fusion(bf16[2,768,240]{1,0,2:T(2,128)(2,1)} %all-reduce.2.cloned.1.call-done), kind=kLoop, calls=%fused_computation.27 | loop fusion | bytes 1474560 | tf_op jit(solution)/shard_map/slice | solution.py:11
  87.9 0.1 fusion.10
  88.0 11.3 %convolution_bitcast_fusion = f32[4096,480]{0,1:T(8,128)} fusion(bf16[1536,4096]{1,0:T(8,128)(2,1)} %bitcast.15, bf16[768,240]{0,1:T(8,128)(2,1)S(1)} %bitcast.16, bf16[768,240]{0,1:T(8,128)(2,1)S(1)} %get-tuple-element.6, bf16[768,240]{0,1:T(8,128)(2,1)S(1)} %get-tuple-element.5), kind=kOutput, calls=%fused_computation.1 | convolution fusion | flops 6045696000 | bytes 21553152 | tf_op jit(solution)/shard_map/dot_general | solution.py:34
  99.3 0.0 reduce-scatter.2.cloned.1.call-update
  99.3 141.0 %reduce-scatter.2.cloned.1.call-done = f32[512,480]{0,1:T(8,128)} async-done(((f32[4096,480]{0,1:T(8,128)}), f32[512,480]{0,1:T(8,128)}) %reduce-scatter.2.cloned.1.call-update) | async-done | bytes 983056 | tf_op jit(solution)/shard_map/reduce_scatter | solution.py:33
  (4 shorter events, 0.1 us)
Async XLA Ops:
  6.5 78.7 %all-reduce.2.cloned.1.call-start = ((), (), s32[]{:S(2)}) async-start(), calls=%async_computation.1 | async-start | bytes 1474560 | tf_op jit(solution)/shard_map/psum | solution.py:29
  7.2 38.2 %copy-start = (f32[768]{0:T(1024)S(1)}, f32[768]{0:T(1024)}, u32[]{:S(2)}) copy-start(f32[768]{0:T(1024)} %param.4) | copy-start | bytes 9220
  48.0 192.4 %reduce-scatter.2.cloned.1.call-start = ((), (), s32[]{:S(2)}) async-start(), calls=%async_computation.2 | async-start | bytes 8847360 | tf_op jit(solution)/shard_map/reduce_scatter | solution.py:33
Sparse Core Ops, SparseCore 0:
  48.1 37.1 all-reduce.1
  99.5 140.8 reduce-scatter.1
where the time goes:
time: 248 us; the launch traced here: 247 us
  waiting for transfers between devices  178 us (72%)
  local copies, waits for them, and re-layouts  40.8 us (16%)
  between operations  14.1 us (6%)
  matrix products  11.3 us (5%)
  other arithmetic  2.62 us (1%)
    reduce_scatter x1, waiting for transfers between devices, body(): lax.psum_scatter(lax.dot_general(sliced, stacked, (((0,), (0,)), ((), ())...  141 us
    psum x1, waiting for transfers between devices, body(): folded = lax.psum(masked.astype(jnp.bfloat16), 'ta')  37.2 us
    unnamed x4, local copies, waits for them, and re-layouts  31.4 us
    dot_general x1, matrix products, body(): lax.dot_general(sliced, stacked, (((0,), (0,)), ((), ())), preferred_elem...  11.3 us
    gather x1, local copies, waits for them, and re-layouts, body(): picked = jnp.take(density, position, axis=2)  6.77 us
  transfers between devices with their start and end apart: 2, of which 2 were waited for; matrix products, arithmetic and copies ran while one was open for 0% of the time, Pallas kernels for 0%

commit v1 on v0

--- a/solution.py
+++ b/solution.py
@@ -1,9 +1,17 @@
+import functools
+
 import jax
 import jax.numpy as jnp
 from jax import lax
+from jax.experimental import pallas as pl
+from jax.experimental.pallas import tpu as pltpu
 from jax.sharding import PartitionSpec as P
 
 RB = 240
+LANES = 128
+CHUNKS = (48, 48, 48, 48, 48)
+ORDERS = ((0, 1, 2), (1, 0, 2), (0, 1, 2), (0, 1, 2), (0, 1, 2))
+MESH = pl.DeviceIdType.MESH
 
 
 def stack_left(folded):
@@ -14,7 +22,7 @@
     return jnp.concatenate([upper_half, lower_half], axis=0)
 
 
-def body(density, coulomb, row_block):
+def plain_body(density, coulomb, row_block):
     local_g = density.shape[1]
     col_width = density.shape[2]
     group_index = lax.axis_index("ta")
@@ -41,7 +49,268 @@
     return kernel.reshape(1, kernel.shape[0], 2, RB)
 
 
+def pick_kernel(local_g, width, window, row_block, density, coulomb, out, held, sem):
+    first = row_block[0] * RB - lax.axis_index("ta") * width
+    start = jnp.minimum(lax.div(jnp.maximum(first, 0), LANES) * LANES, width - window)
+    start = pl.multiple_of(start, LANES)
+    copy = pltpu.make_async_copy(density.at[:, pl.ds(start, window)], held, sem)
+    copy.start()
+    row = lax.broadcasted_iota(jnp.int32, (RB, window), 0)
+    column = lax.broadcasted_iota(jnp.int32, (RB, window), 1)
+    chosen = jnp.where(start + column == first + row, 1.0, 0.0).astype(jnp.bfloat16)
+    copy.wait()
+    for part in range(2):
+        picked = lax.dot_general(
+            chosen,
+            held[part * local_g : (part + 1) * local_g, :],
+            (((1,), (1,)), ((), ())),
+            preferred_element_type=jnp.float32,
+        )
+        out[part] = (coulomb[...] * picked).astype(jnp.bfloat16)
+
+
+def flipped(index, bit):
+    step = 2**bit
+    return index + step * (1 - 2 * lax.rem(lax.div(index, step), 2))
+
+
+def exchange_kernel(
+    n_ga, local_g, own,
+    masked, density, out,
+    dens, half, other_half, far_half, full, lhs, acc, s0, r0, s1, r1, s2, r2,
+    dens_sem, core_ss, core_rs, far_ss, far_rs, back_ss, back_rs,
+    ss0, rs0, ss1, rs1, ss2, rs2,
+):
+    ga = lax.axis_index("ga")
+    ta = lax.axis_index("ta")
+    core = lax.rem(ta, 2)
+    core_peer = {"ta": flipped(ta, 0)}
+    far_peer = {"ta": flipped(ta, 1)}
+    ga_peer = [{"ga": flipped(ga, bit)} for bit in range(3)]
+    offsets = [sum(CHUNKS[:c]) for c in range(len(CHUNKS))]
+
+    def block_of(relative_bits):
+        index = ga
+        for bit, flag in enumerate(relative_bits):
+            step = 2**bit
+            index = index + flag * step * (1 - 2 * lax.rem(lax.div(ga, step), 2))
+        return index
+
+    def load(r):
+        bits = [lax.rem(lax.div(r, 2**bit), 2) for bit in range(3)]
+        column = pl.multiple_of(block_of(bits) * own, own)
+        return pltpu.make_async_copy(density.at[:, pl.ds(column, own)], dens.at[r], dens_sem.at[r])
+
+    def start_load(i, carry):
+        load(7 - i).start()
+        return carry
+
+    lax.fori_loop(0, n_ga, start_load, 0)
+
+    barrier = pltpu.get_barrier_semaphore()
+    peers = [core_peer, far_peer] + ga_peer
+    for peer in peers:
+        pl.semaphore_signal(barrier, inc=1, device_id=peer, device_id_type=MESH)
+    pl.semaphore_wait(barrier, len(peers))
+
+    def remote(src, dst, send, recv, peer):
+        return pltpu.make_async_remote_copy(
+            src_ref=src, dst_ref=dst, send_sem=send, recv_sem=recv,
+            device_id=peer, device_id_type=MESH,
+        )
+
+    to_core = remote(masked.at[1 - core], other_half, core_ss, core_rs, core_peer)
+    to_core.start()
+
+    def to_far(c):
+        rows = pl.ds(offsets[c], CHUNKS[c])
+        return remote(half.at[rows], far_half.at[rows], far_ss.at[c], far_rs.at[c], far_peer)
+
+    def back(c, part):
+        rows = pl.ds(offsets[c], CHUNKS[c])
+        view = full.at[part, rows]
+        return remote(view, view, back_ss.at[c], back_rs.at[c], core_peer)
+
+    to_core.wait_recv()
+    f32 = jnp.float32
+    for c, size in enumerate(CHUNKS):
+        rows = pl.ds(offsets[c], size)
+        half[rows] = (masked[core, rows].astype(f32) + other_half[rows].astype(f32)).astype(jnp.bfloat16)
+        to_far(c).start()
+
+    def prepare(c):
+        rows = pl.ds(offsets[c], CHUNKS[c])
+        to_far(c).wait_recv()
+        full[core, rows] = (half[rows].astype(f32) + far_half[rows].astype(f32)).astype(jnp.bfloat16)
+        back(c, core).start()
+
+    def both(c):
+        return pl.ds(2 * offsets[c], 2 * CHUNKS[c])
+
+    def send0(c, q):
+        view = both(c)
+        sem = 4 * c + q
+        return remote(s0.at[q, view], r0.at[q, view], ss0.at[sem], rs0.at[sem], ga_peer[ORDERS[c][0]])
+
+    def send1(c, k):
+        view = both(c)
+        sem = 2 * c + k
+        return remote(s1.at[k, view], r1.at[k, view], ss1.at[sem], rs1.at[sem], ga_peer[ORDERS[c][1]])
+
+    def send2(c):
+        view = both(c)
+        return remote(s2.at[view], r2.at[view], ss2.at[c], rs2.at[c], ga_peer[ORDERS[c][2]])
+
+    def base(c, q):
+        _, second, third = ORDERS[c]
+        return 2**second * (1 - lax.div(q, 2)) + 2**third * (1 - lax.rem(q, 2))
+
+    def product(c, r):
+        return jnp.dot(lhs[both(c)], dens[r], preferred_element_type=f32)
+
+    def fill_left(c):
+        rows = pl.ds(offsets[c], CHUNKS[c])
+        back(c, 1 - core).wait_recv()
+        real_part = full[0, rows]
+        imag_part = full[1, rows]
+        upper = pl.ds(2 * offsets[c], CHUNKS[c])
+        lower = pl.ds(2 * offsets[c] + CHUNKS[c], CHUNKS[c])
+        lhs[upper, 0:local_g] = real_part
+        lhs[upper, local_g : 2 * local_g] = imag_part
+        lhs[lower, 0:local_g] = -imag_part
+        lhs[lower, local_g : 2 * local_g] = real_part
+
+    def sent_products(c):
+        def step(q, carry):
+            r = base(c, q) + 2 ** ORDERS[c][0]
+            if c == 0:
+                load(r).wait()
+            s0[q, both(c)] = product(c, r).astype(jnp.bfloat16)
+            send0(c, q).start()
+            return carry
+
+        lax.fori_loop(0, 4, step, 0)
+
+    def kept_products(c):
+        def step(q, carry):
+            r = base(c, q)
+            if c == 0:
+                load(r).wait()
+            acc[q, both(c)] = product(c, r)
+            return carry
+
+        lax.fori_loop(0, 4, step, 0)
+
+    def second_stage(c):
+        view = both(c)
+        for k in range(2):
+            send0(c, k).wait_recv()
+            s1[k, view] = (acc[k, view] + r0[k, view].astype(f32)).astype(jnp.bfloat16)
+            send1(c, k).start()
+
+    def third_stage(c):
+        view = both(c)
+        send0(c, 2).wait_recv()
+        send1(c, 0).wait_recv()
+        s2[view] = (acc[2, view] + r0[2, view].astype(f32) + r1[0, view].astype(f32)).astype(jnp.bfloat16)
+        send2(c).start()
+
+    def last_stage(c):
+        send0(c, 3).wait_recv()
+        send1(c, 1).wait_recv()
+        send2(c).wait_recv()
+        for part in range(2):
+            view = pl.ds(2 * offsets[c] + part * CHUNKS[c], CHUNKS[c])
+            out[part, pl.ds(offsets[c], CHUNKS[c])] = (
+                acc[3, view] + r0[3, view].astype(f32) + r1[1, view].astype(f32) + r2[view].astype(f32)
+            )
+
+    count = len(CHUNKS)
+    prepare(0)
+    for c in range(count + 3):
+        if c < count:
+            fill_left(c)
+            sent_products(c)
+            if c + 1 < count:
+                prepare(c + 1)
+            kept_products(c)
+        if 0 <= c - 1 < count:
+            second_stage(c - 1)
+        if 0 <= c - 2 < count:
+            third_stage(c - 2)
+        if 0 <= c - 3 < count:
+            last_stage(c - 3)
+
+    to_core.wait_send()
+    for c in range(count):
+        to_far(c).wait_send()
+        back(c, core).wait_send()
+        for q in range(4):
+            send0(c, q).wait_send()
+        for k in range(2):
+            send1(c, k).wait_send()
+        send2(c).wait_send()
+
+
+def kernel_body(n_ga, density, coulomb, row_block):
+    local_g = density.shape[1]
+    width = density.shape[2]
+    own = width // n_ga
+    flat = density.reshape(2 * local_g, width)
+    window = -(-(RB + LANES - 1) // LANES) * LANES
+    bf16, f32 = jnp.bfloat16, jnp.float32
+    vmem, anywhere = pl.BlockSpec(memory_space=pltpu.VMEM), pl.BlockSpec(memory_space=pl.ANY)
+    masked = pl.pallas_call(
+        functools.partial(pick_kernel, local_g, width, window),
+        out_shape=jax.ShapeDtypeStruct((2, RB, local_g), bf16),
+        in_specs=[pl.BlockSpec(memory_space=pltpu.SMEM), anywhere, vmem],
+        out_specs=vmem,
+        scratch_shapes=[pltpu.VMEM((2 * local_g, window), bf16), pltpu.SemaphoreType.DMA],
+    )(row_block, flat, coulomb.reshape(1, local_g))
+    count = len(CHUNKS)
+    dma = pltpu.SemaphoreType.DMA
+    kernel = pl.pallas_call(
+        functools.partial(exchange_kernel, n_ga, local_g, own),
+        out_shape=jax.ShapeDtypeStruct((2, RB, own), f32),
+        in_specs=[vmem, anywhere],
+        out_specs=vmem,
+        scratch_shapes=[
+            pltpu.VMEM((n_ga, 2 * local_g, own), bf16),
+            pltpu.VMEM((RB, local_g), bf16),
+            pltpu.VMEM((RB, local_g), bf16),
+            pltpu.VMEM((RB, local_g), bf16),
+            pltpu.VMEM((2, RB, local_g), bf16),
+            pltpu.VMEM((2 * RB, 2 * local_g), bf16),
+            pltpu.VMEM((4, 2 * RB, own), f32),
+            pltpu.VMEM((4, 2 * RB, own), bf16),
+            pltpu.VMEM((4, 2 * RB, own), bf16),
+            pltpu.VMEM((2, 2 * RB, own), bf16),
+            pltpu.VMEM((2, 2 * RB, own), bf16),
+            pltpu.VMEM((2 * RB, own), bf16),
+            pltpu.VMEM((2 * RB, own), bf16),
+            dma((n_ga,)),
+            dma, dma,
+            dma((count,)), dma((count,)),
+            dma((count,)), dma((count,)),
+            dma((4 * count,)), dma((4 * count,)),
+            dma((2 * count,)), dma((2 * count,)),
+            dma((count,)), dma((count,)),
+        ],
+        compiler_params=pltpu.CompilerParams(collective_id=0, has_side_effects=True),
+    )(masked, flat)
+    return jnp.transpose(kernel, (2, 0, 1))[None]
+
+
 def solution(mesh):
     in_specs = (P(None, "ga", "ta"), P("ga"), P())
     out_specs = P("ta", "ga", None, None)
+    n_ga, n_ta = mesh.shape["ga"], mesh.shape["ta"]
+
+    def body(density, coulomb, row_block):
+        _, local_g, width = density.shape
+        aligned = local_g % LANES == 0 and width % (n_ga * LANES) == 0
+        if aligned and n_ga == 8 and n_ta == 4:
+            return kernel_body(n_ga, density, coulomb, row_block)
+        return plain_body(density, coulomb, row_block)
+
     return jax.shard_map(body, mesh=mesh, in_specs=in_specs, out_specs=out_specs, check_vma=False)

time: 248 us -> 69.3 us (0.28)
  waiting for transfers between devices: 178 us -> 0 us
  Pallas kernels: 0 us -> 64.8 us
  local copies, waits for them, and re-layouts: 40.8 us -> 3.49 us
  between operations: 14.1 us -> 0.67 us
  matrix products: 11.3 us -> 0 us
  other arithmetic: 2.62 us -> 0 us
    reduce_scatter x1 -> x0, waiting for transfers between devices: 141 us -> none  [body(): lax.psum_scatter(lax.dot_general(sliced, stacked, (((0,), (0,)), ((), ())...]
    pallas_call x0 -> x2, Pallas kernels: none -> 64.8 us  [the longest x1 61.4 us: kernel_body(): pl.pallas_call(functools.partial(exchange_kernel, n_ga, local_g, own), ou...]
    psum x1 -> x0, waiting for transfers between devices: 37.2 us -> none  [body(): folded = lax.psum(masked.astype(jnp.bfloat16), 'ta')]
    unnamed x4 -> x1, local copies, waits for them, and re-layouts: 31.4 us -> 2.21 us
    dot_general x1 -> x0, matrix products: 11.3 us -> none  [body(): lax.dot_general(sliced, stacked, (((0,), (0,)), ((), ())), preferred_elem...]
    gather x1 -> x0, local copies, waits for them, and re-layouts: 6.77 us -> none  [body(): picked = jnp.take(density, position, axis=2)]
    slice x1 -> x0, local copies, waits for them, and re-layouts: 2.61 us -> none  [stack_left(): imag_part = folded[1]]
    convert_element_type x1 -> x0, other arithmetic: 2.52 us -> none  [body(): folded = lax.psum(masked.astype(jnp.bfloat16), 'ta')]
  transfers between devices with their start and end apart: 2 -> 0, of which waited for: 2 -> 0; matrix products, arithmetic and copies ran while one was open for 0% -> 0% of each run, Pallas kernels for 0% -> 0%
where the time goes in v1:
time: 69.3 us; the launch traced here: 69 us
  Pallas kernels  64.8 us (94%)
  local copies, waits for them, and re-layouts  3.49 us (5%)
    pallas_call x1, Pallas kernels, kernel_body(): pl.pallas_call(functools.partial(exchange_kernel, n_ga, local_g, own), ou...  61.4 us
    pallas_call x1, Pallas kernels, kernel_body(): pl.pallas_call(functools.partial(pick_kernel, local_g, width, window), ou...  3.42 us
    unnamed x1, local copies, waits for them, and re-layouts  2.21 us

profile of v1, /device:TPU:0, one launch (start us, length us, event | category | flops | bytes accessed | tf_op | source)
XLA Modules:
  0.0 69.0 jit_solution(13446297358998659217)
XLA Ops:
  0.7 1.3 %reshape.7.coulomb = f32[1,768]{1,0:T(1,128)} reshape(f32[768]{0:T(1024)} %param.4) | data formatting | bytes 6144 | tf_op jit(solution)/shard_map/reshape | solution.py:269
  1.9 3.4 %shard_map.37.masked = bf16[2,240,768]{2,1,0:T(8,128)(2,1)} custom-call(s32[1]{0:T(128)S(6)} %copy.5.row_block, bf16[1536,4096]{1,0:T(8,128)(2,1)} %bitcast.4, f32[1,768]{1,0:T(1,128)} %reshape.7.coulomb), custom_call_target="tpu_custom_call" | custom-call | tf_op jit(solution)/shard_map/pallas_call | solution.py:263
  5.4 61.4 %shard_map.38 = f32[2,240,512]{2,1,0:T(8,128)} custom-call(bf16[2,240,768]{2,1,0:T(8,128)(2,1)} %shard_map.37.masked, bf16[1536,4096]{1,0:T(8,128)(2,1)} %bitcast.5), custom_call_target="tpu_custom_call" | custom-call | tf_op jit(solution)/shard_map/pallas_call | solution.py:272
  66.8 2.2 %copy.6 = f32[1,512,2,240]{1,3,2,0:T(8,128)} copy(f32[1,512,2,240]{1,3,2,0:T(8,128)} %bitcast.6) | data formatting | bytes 1966080

commit v2 on v1

--- a/solution.py
+++ b/solution.py
@@ -12,6 +12,9 @@
 CHUNKS = (48, 48, 48, 48, 48)
 ORDERS = ((0, 1, 2), (1, 0, 2), (0, 1, 2), (0, 1, 2), (0, 1, 2))
 MESH = pl.DeviceIdType.MESH
+VMEM_BYTES = 56 * 2**20
+PICK_BYTES = 56 * 2**20
+LAGS = (1, 2, 3)
 
 
 def stack_left(folded):
@@ -66,7 +69,7 @@
             (((1,), (1,)), ((), ())),
             preferred_element_type=jnp.float32,
         )
-        out[part] = (coulomb[...] * picked).astype(jnp.bfloat16)
+        out[part] = (coulomb[...][None, :] * picked).astype(jnp.bfloat16)
 
 
 def flipped(index, bit):
@@ -119,8 +122,14 @@
             device_id=peer, device_id_type=MESH,
         )
 
-    to_core = remote(masked.at[1 - core], other_half, core_ss, core_rs, core_peer)
-    to_core.start()
+    def to_core(c):
+        rows = pl.ds(offsets[c], CHUNKS[c])
+        return remote(
+            masked.at[1 - core, rows], other_half.at[rows], core_ss.at[c], core_rs.at[c], core_peer
+        )
+
+    for c in range(len(CHUNKS)):
+        to_core(c).start()
 
     def to_far(c):
         rows = pl.ds(offsets[c], CHUNKS[c])
@@ -131,10 +140,10 @@
         view = full.at[part, rows]
         return remote(view, view, back_ss.at[c], back_rs.at[c], core_peer)
 
-    to_core.wait_recv()
     f32 = jnp.float32
     for c, size in enumerate(CHUNKS):
         rows = pl.ds(offsets[c], size)
+        to_core(c).wait_recv()
         half[rows] = (masked[core, rows].astype(f32) + other_half[rows].astype(f32)).astype(jnp.bfloat16)
         to_far(c).start()
 
@@ -227,22 +236,22 @@
 
     count = len(CHUNKS)
     prepare(0)
-    for c in range(count + 3):
+    for c in range(count + LAGS[2]):
         if c < count:
             fill_left(c)
             sent_products(c)
             if c + 1 < count:
                 prepare(c + 1)
             kept_products(c)
-        if 0 <= c - 1 < count:
-            second_stage(c - 1)
-        if 0 <= c - 2 < count:
-            third_stage(c - 2)
-        if 0 <= c - 3 < count:
-            last_stage(c - 3)
-
-    to_core.wait_send()
+        if 0 <= c - LAGS[0] < count:
+            second_stage(c - LAGS[0])
+        if 0 <= c - LAGS[1] < count:
+            third_stage(c - LAGS[1])
+        if 0 <= c - LAGS[2] < count:
+            last_stage(c - LAGS[2])
+
     for c in range(count):
+        to_core(c).wait_send()
         to_far(c).wait_send()
         back(c, core).wait_send()
         for q in range(4):
@@ -266,7 +275,8 @@
         in_specs=[pl.BlockSpec(memory_space=pltpu.SMEM), anywhere, vmem],
         out_specs=vmem,
         scratch_shapes=[pltpu.VMEM((2 * local_g, window), bf16), pltpu.SemaphoreType.DMA],
-    )(row_block, flat, coulomb.reshape(1, local_g))
+        compiler_params=pltpu.CompilerParams(vmem_limit_bytes=PICK_BYTES),
+    )(row_block, flat, coulomb)
     count = len(CHUNKS)
     dma = pltpu.SemaphoreType.DMA
     kernel = pl.pallas_call(
@@ -289,14 +299,16 @@
             pltpu.VMEM((2 * RB, own), bf16),
             pltpu.VMEM((2 * RB, own), bf16),
             dma((n_ga,)),
-            dma, dma,
+            dma((count,)), dma((count,)),
             dma((count,)), dma((count,)),
             dma((count,)), dma((count,)),
             dma((4 * count,)), dma((4 * count,)),
             dma((2 * count,)), dma((2 * count,)),
             dma((count,)), dma((count,)),
         ],
-        compiler_params=pltpu.CompilerParams(collective_id=0, has_side_effects=True),
+        compiler_params=pltpu.CompilerParams(
+            collective_id=0, has_side_effects=True, vmem_limit_bytes=VMEM_BYTES
+        ),
     )(masked, flat)
     return jnp.transpose(kernel, (2, 0, 1))[None]
 

time: 69.3 us -> 67.6 us (0.975)
  local copies, waits for them, and re-layouts: 3.49 us -> 2.21 us
    reshape x1 -> x0, local copies, waits for them, and re-layouts: 1.28 us -> none  [kernel_body(): coulomb.reshape(1, local_g)]
where the time goes in v2:
time: 67.6 us; the launch traced here: 67.3 us
  Pallas kernels  64.5 us (95%)
  local copies, waits for them, and re-layouts  2.21 us (3%)
    pallas_call x1, Pallas kernels, kernel_body(): pl.pallas_call(functools.partial(exchange_kernel, n_ga, local_g, own), ou...  61 us
    pallas_call x1, Pallas kernels, kernel_body(): pl.pallas_call(functools.partial(pick_kernel, local_g, width, window), ou...  3.43 us
    unnamed x1, local copies, waits for them, and re-layouts  2.21 us

profile of v2, /device:TPU:0, one launch (start us, length us, event | category | flops | bytes accessed | tf_op | source)
XLA Modules:
  0.0 67.3 jit_solution(6338627388199385414)
XLA Ops:
  0.7 3.4 %shard_map.37.masked = bf16[2,240,768]{2,1,0:T(8,128)(2,1)} custom-call(s32[1]{0:T(128)S(6)} %copy.5.row_block, bf16[1536,4096]{1,0:T(8,128)(2,1)} %bitcast.4, f32[768]{0:T(1024)} %coulomb.1), custom_call_target="tpu_custom_call" | custom-call | tf_op jit(solution)/shard_map/pallas_call | solution.py:272
  4.1 61.0 %shard_map.38 = f32[2,240,512]{2,1,0:T(8,128)} custom-call(bf16[2,240,768]{2,1,0:T(8,128)(2,1)} %shard_map.37.masked, bf16[1536,4096]{1,0:T(8,128)(2,1)} %bitcast.5), custom_call_target="tpu_custom_call" | custom-call | tf_op jit(solution)/shard_map/pallas_call | solution.py:282
  65.1 2.2 %copy.6 = f32[1,512,2,240]{1,3,2,0:T(8,128)} copy(f32[1,512,2,240]{1,3,2,0:T(8,128)} %bitcast.6) | data formatting | bytes 1966080
